TPU v7x, 32 devices: a whole 2x2x4 slice. The times are simulated.
32 devices in a mesh: grp: 4 (over z), sp: 8 (over y, x, core).
Axes of the slice: x: 2, y: 2, z: 4, core: 2. Of those that a mesh axis runs over, the one named last changes fastest.
Arguments:
- tokens: bfloat16 [2048, 2880], P(('grp', 'sp')), may hold values from -36 to 36
- query_weight: bfloat16 [2880, 2048], P(None, 'sp'), may hold values from -0.109375 to 0.109375
- key_value_weight: bfloat16 [2880, 1024], replicated, may hold values from -0.109375 to 0.109375
- block_places: int32 [16], replicated, may hold values from 0 to 15, each once
- sinks: float32 [32], replicated, may hold values from -1 to 5
Outputs:
- attended: bfloat16 [2048, 2048], P(('grp', 'sp'))
Inputs may be any that keep to these rules, and one draw needn't show every extreme that they name: `block_places`: every sequence block appears once.
All inputs are finite; a program needn't handle non-finite values.
Results may differ from a plain program's by a relative error of at most 0.008.
The roundings to bfloat16 on the way count: a program that leaves them out, or rounds other values in their place, can miss the bound.
Values may be sent and summed in bfloat16 or wider, within the bound.
A program may use at most 128 MiB of HBM per device.

v0:
```python
import jax
import jax.numpy as jnp
from jax import lax
from jax.sharding import PartitionSpec as P

QUERY_HEADS = 32
HEAD_SIZE = 64
BPG = 4


rope_base = 150000.0
neg_large = -1e30


def rotate(vectors, angles):
    middle = vectors.shape[-1] // 2
    first_half = vectors[..., :middle]
    second_half = vectors[..., middle:]
    cosine = jnp.cos(angles)
    sine_part = jnp.sin(angles)
    return jnp.concatenate(
        [
            first_half * cosine - second_half * sine_part,
            second_half * cosine + first_half * sine_part,
        ],
        axis=-1,
    )


def locate(stored, block_rows, block_places):
    blocks = stored // block_rows
    table = jnp.arange(block_places.shape[0], dtype=jnp.int32)
    onehot = (blocks[:, None] == table[None, :]).astype(jnp.int32)
    return jnp.sum(onehot * block_places[None, :], axis=1) * block_rows + stored % block_rows


def prepare(projected, own_places, query_cols, kv_cols, head_count):
    row_count = projected.shape[0]
    inverse = rope_base ** (-(jnp.arange(HEAD_SIZE // 2, dtype=jnp.float32) * 2.0) / HEAD_SIZE)
    angles = own_places.astype(jnp.float32)[:, None, None] * inverse[None, None, :]
    queries = rotate(
        projected[:, :query_cols].reshape(row_count, query_cols // HEAD_SIZE, HEAD_SIZE), angles
    ).astype(jnp.bfloat16)
    rotated_keys = rotate(
        projected[:, query_cols : query_cols + kv_cols].reshape(row_count, head_count, HEAD_SIZE),
        angles,
    )
    key_value_pair = jnp.concatenate(
        [rotated_keys.reshape(row_count, kv_cols), projected[:, query_cols + kv_cols :]], axis=1
    ).astype(jnp.bfloat16)
    return (queries, key_value_pair)


def attend(state, queries, query_places, key_value_pair, key_places, head_count):
    maxima, totals, mixture = state
    key_count = key_value_pair.shape[0]
    column_half = key_value_pair.shape[1] // 2
    key_part = key_value_pair[:, :column_half].reshape(key_count, head_count, HEAD_SIZE)
    value_part = key_value_pair[:, column_half:].reshape(key_count, head_count, HEAD_SIZE)
    scores = jnp.einsum(
        "qhgd,khd->hgqk", queries, key_part, preferred_element_type=jnp.float32
    ) * HEAD_SIZE ** (-0.5)
    allowed = key_places[None, :] <= query_places[:, None]
    scores = jnp.where(allowed, scores, neg_large)
    updated = jnp.maximum(maxima, jnp.max(scores, axis=-1))
    weights = jnp.where(allowed, jnp.exp(scores - updated[..., None]), 0.0)
    factor = jnp.exp(maxima - updated)
    totals = totals * factor + jnp.sum(weights, axis=-1)
    mixture = mixture * factor[..., None] + jnp.einsum(
        "hgqk,khd->hgqd",
        weights.astype(jnp.bfloat16),
        value_part,
        preferred_element_type=jnp.float32,
    )
    return (updated, totals, mixture)


def per_device(tokens, query_weight, key_value_weight, block_places, sinks):
    sp_count = lax.axis_size("sp")
    local_rows = tokens.shape[0]
    group_rows = local_rows * sp_count
    block_rows = group_rows // BPG
    kv_total = key_value_weight.shape[1] // (2 * HEAD_SIZE)
    sp_place = lax.axis_index("sp")
    grp_place = lax.axis_index("grp")
    query_cols = query_weight.shape[1]
    query_heads = query_cols // HEAD_SIZE
    head_count = max(kv_total // sp_count, 1)
    kv_cols = head_count * HEAD_SIZE
    first_head = sp_place * query_heads // (QUERY_HEADS // kv_total)
    key_weight = lax.dynamic_slice_in_dim(key_value_weight, first_head * HEAD_SIZE, kv_cols, 1)
    value_weight = lax.dynamic_slice_in_dim(
        key_value_weight, kv_total * HEAD_SIZE + first_head * HEAD_SIZE, kv_cols, 1
    )
    joined = jnp.concatenate([query_weight, key_weight, value_weight], axis=1)
    projected = jnp.dot(
        lax.all_gather(tokens, "sp", axis=0, tiled=True), joined, preferred_element_type=jnp.float32
    )
    query_local = jnp.arange(group_rows, dtype=jnp.int32)
    head_first = sp_place * query_heads
    own_places = locate(grp_place * group_rows + query_local, block_rows, block_places)
    queries, key_value_pair = prepare(projected, own_places, query_cols, kv_cols, head_count)
    query_sharing = query_heads // head_count
    head_sinks = lax.dynamic_slice_in_dim(sinks, head_first, query_heads, 0).reshape(
        head_count, query_sharing
    )
    sink_rows = jnp.broadcast_to(head_sinks[:, :, None], (head_count, query_sharing, group_rows))
    query_block4 = queries.reshape(group_rows, head_count, query_sharing, HEAD_SIZE)
    initial = (
        sink_rows,
        jnp.ones((head_count, query_sharing, group_rows), jnp.float32),
        jnp.zeros((head_count, query_sharing, group_rows, HEAD_SIZE), jnp.float32),
    )
    piece = lax.all_gather(key_value_pair, "grp", axis=0, tiled=True)
    step_rows = min(piece.shape[0], group_rows)
    turns = piece.shape[0] // step_rows

    def visit(turn, inner):
        offset = turn * step_rows
        piece_rows = lax.dynamic_slice_in_dim(piece, offset, step_rows, 0)
        position = offset + jnp.arange(step_rows, dtype=jnp.int32)
        stored = position // group_rows * group_rows + position % group_rows
        key_places = locate(stored, block_rows, block_places)
        return attend(inner, query_block4, own_places, piece_rows, key_places, head_count)

    maxima, totals, mixture = lax.fori_loop(0, turns, visit, initial)
    normed = jnp.transpose(mixture, (2, 0, 1, 3)) / jnp.transpose(totals, (2, 0, 1))[..., None]
    attended = normed.reshape(group_rows, query_cols).astype(jnp.bfloat16)
    return lax.all_to_all(attended, "sp", split_axis=0, concat_axis=1, tiled=True)


def solution(mesh):
    in_specs = (P(("grp", "sp"), None), P(None, "sp"), P(), P(), P())
    out_specs = P(("grp", "sp"), None)
    return jax.shard_map(
        per_device, mesh=mesh, in_specs=in_specs, out_specs=out_specs, check_vma=False
    )
```

profile of v0, /device:TPU:0, one launch (start us, length us, event | category | flops | bytes accessed | tf_op | source)
XLA Modules:
  0.0 114.0 jit_solution(16821734951300925589)
XLA Ops:
  6.5 0.0 all-gather.2.cloned.1.call-start
  6.5 0.7 all-gather.2.cloned.1.call-update
  7.3 0.7 dynamic_slice.20
  8.1 0.7 select_reduce_fusion.1
  8.8 0.3 multiply_cosine_fusion
  9.1 1.8 %constant_dynamic-slice_fusion.1 = (bf16[2880,64]{1,0:T(8,128)(2,1)S(1)}, bf16[2880,64]{1,0:T(8,128)(2,1)S(1)}) fusion(bf16[2880,1024]{1,0:T(8,128)(2,1)} %param.9, s32[]{:T(128)S(6)} %select_n.163, s32[]{:T(128)S(6)} %select_n.164), kind=kLoop, calls=%fused_computation.92 | loop fusion | bytes 1474568 | tf_op jit(solution)/shard_map/dynamic_slice | solution.py:91
  11.0 32.6 %all-gather.2.cloned.1.call-done = bf16[512,2880]{1,0:T(8,128)(2,1)} async-done(((bf16[64,2880]{1,0:T(8,128)(2,1)}), bf16[512,2880]{1,0:T(8,128)(2,1)}) %all-gather.2.cloned.1.call-update) | async-done | bytes 2949136 | tf_op jit(solution)/shard_map/all_gather | solution.py:97
  43.6 0.0 copy-start.1
  43.6 4.1 %fusion.32 = f32[512,384]{0,1:T(8,128)S(1)} fusion(bf16[512,2880]{1,0:T(8,128)(2,1)} %all-gather.2.cloned.1.call-done, bf16[2880,64]{1,0:T(8,128)(2,1)S(1)} %get-tuple-element.296, bf16[2880,64]{1,0:T(8,128)(2,1)S(1)} %get-tuple-element.295, bf16[2880,256]{1,0:T(8,128)(2,1)} %param.8), kind=kOutput, calls=%fused_computation.53 | convolution fusion | flops 1139097600 | bytes 5947392 | tf_op jit(solution)/shard_map/dot_general | solution.py:96
  47.8 0.3 fusion.43
  48.2 16.0 %all_gather.7 = bf16[2048,128]{0,1:T(8,128)(2,1)S(1)} all-gather(bf16[512,128]{0,1:T(8,128)(2,1)S(1)} %pad_maximum_fusion.1), channel_id=1, replica_groups=mesh['grp'=4,'sp'=8] {'grp'}, dimensions={0}, use_global_device_ids=true | all-gather | bytes 655360 | tf_op jit(solution)/shard_map/all_gather | solution.py:114
  64.2 0.1 fusion.36
  64.3 0.1 broadcast_in_dim.74
  64.4 0.0 copy-done.1
  64.4 31.9 %while.21 = (s32[]{:T(128)}, f32[1,4,512]{2,1,0:T(4,128)S(1)}, f32[1,4,512]{2,1,0:T(4,128)S(1)}, f32[1,4,512,64]{2,3,1,0:T(8,128)S(1)}, s32[16]{0:T(128)S(1)}, /...) while((s32[]{:T(128)}, f32[1,4,512]{2,1,0:T(4,128)S(1)}, ...), condition=%wide.region_5.6_spmd.clone, body=%wide.region_1.5_spmd.clone.sunk | while | flops 282791424 | bytes 31996208 | solution.py:126
  64.4 0.1 select_reduce_fusion.3
  64.5 0.2 broadcast_compare_fusion.3
  64.7 2.8 %fusion.62 = (f32[4,512]{1,0:T(4,128)S(1)}, f32[512,512,4]{1,0,2:T(8,128)}) fusion(pred[512,512]{0,1:T(8,128)(4,1)S(1)} %broadcast_compare_fusion.3, bf16[512,1,4,64]{0,3,2,1:T(8,128)(2,1)S(1)} %get-tuple-element.393, bf16[2048,128]{0,1:T(8,128)(2,1)S(1)} %get-tuple-element.392, s32[]{:T(128)S(6)} %select_n.256), kind=kOutput, calls=%fused_computation.2.clone.1 | convolution fusion | flops 137361408 | bytes 4792324 | tf_op jit(solution)/shard_map/while/body/eval_jaxpr/qhgd,khd->hgqk/dot_general | solution.py:60
  67.5 0.0 copy-start
  67.6 3.7 %fusion.65 = f32[1,4,512,64]{2,3,1,0:T(8,128)S(1)} fusion(f32[512,512,4]{1,0,2:T(8,128)} %get-tuple-element.358, f32[4,512]{1,0:T(4,128)S(1)} %bitcast.99, pred[512,512]{0,1:T(8,128)(4,1)S(1)} %broadcast_compare_fusion.3, f32[1,4,512,64]{2,3,1,0:T(8,128)S(1)} %get-tuple-element.376, f32[4,512]{1,0:T(4,128)S(1)} %get-tuple-element.359, ...), kind=kOutput, calls=%fused_computation.9.clone.1 | convolution fusion | flops 139853824 | bytes 5586953 | tf_op jit(solution)/shard_map/while/body/eval_jaxpr/hgqk,khd->hgqd/dot_general | solution.py:69
  71.3 0.0 copy-done
  71.3 1.0 fusion.64
  72.4 0.1 select_reduce_fusion.3
  72.5 0.2 broadcast_compare_fusion.3
  72.7 2.8 %fusion.62 = (f32[4,512]{1,0:T(4,128)S(1)}, f32[512,512,4]{1,0,2:T(8,128)}) fusion(pred[512,512]{0,1:T(8,128)(4,1)S(1)} %broadcast_compare_fusion.3, bf16[512,1,4,64]{0,3,2,1:T(8,128)(2,1)S(1)} %get-tuple-element.393, bf16[2048,128]{0,1:T(8,128)(2,1)S(1)} %get-tuple-element.392, s32[]{:T(128)S(6)} %select_n.256), kind=kOutput, calls=%fused_computation.2.clone.1 | convolution fusion | flops 137361408 | bytes 4792324 | tf_op jit(solution)/shard_map/while/body/eval_jaxpr/qhgd,khd->hgqk/dot_general | solution.py:60
  75.5 0.0 copy-start
  75.6 3.7 %fusion.65 = f32[1,4,512,64]{2,3,1,0:T(8,128)S(1)} fusion(f32[512,512,4]{1,0,2:T(8,128)} %get-tuple-element.358, f32[4,512]{1,0:T(4,128)S(1)} %bitcast.99, pred[512,512]{0,1:T(8,128)(4,1)S(1)} %broadcast_compare_fusion.3, f32[1,4,512,64]{2,3,1,0:T(8,128)S(1)} %get-tuple-element.376, f32[4,512]{1,0:T(4,128)S(1)} %get-tuple-element.359, ...), kind=kOutput, calls=%fused_computation.9.clone.1 | convolution fusion | flops 139853824 | bytes 5586953 | tf_op jit(solution)/shard_map/while/body/eval_jaxpr/hgqk,khd->hgqd/dot_general | solution.py:69
  79.3 0.0 copy-done
  79.3 1.0 fusion.64
  80.4 0.1 select_reduce_fusion.3
  80.5 0.2 broadcast_compare_fusion.3
  80.7 2.8 %fusion.62 = (f32[4,512]{1,0:T(4,128)S(1)}, f32[512,512,4]{1,0,2:T(8,128)}) fusion(pred[512,512]{0,1:T(8,128)(4,1)S(1)} %broadcast_compare_fusion.3, bf16[512,1,4,64]{0,3,2,1:T(8,128)(2,1)S(1)} %get-tuple-element.393, bf16[2048,128]{0,1:T(8,128)(2,1)S(1)} %get-tuple-element.392, s32[]{:T(128)S(6)} %select_n.256), kind=kOutput, calls=%fused_computation.2.clone.1 | convolution fusion | flops 137361408 | bytes 4792324 | tf_op jit(solution)/shard_map/while/body/eval_jaxpr/qhgd,khd->hgqk/dot_general | solution.py:60
  83.5 0.0 copy-start
  83.5 3.7 %fusion.65 = f32[1,4,512,64]{2,3,1,0:T(8,128)S(1)} fusion(f32[512,512,4]{1,0,2:T(8,128)} %get-tuple-element.358, f32[4,512]{1,0:T(4,128)S(1)} %bitcast.99, pred[512,512]{0,1:T(8,128)(4,1)S(1)} %broadcast_compare_fusion.3, f32[1,4,512,64]{2,3,1,0:T(8,128)S(1)} %get-tuple-element.376, f32[4,512]{1,0:T(4,128)S(1)} %get-tuple-element.359, ...), kind=kOutput, calls=%fused_computation.9.clone.1 | convolution fusion | flops 139853824 | bytes 5586953 | tf_op jit(solution)/shard_map/while/body/eval_jaxpr/hgqk,khd->hgqd/dot_general | solution.py:69
  87.2 0.0 copy-done
  87.3 1.0 fusion.64
  88.4 0.1 select_reduce_fusion.3
  88.5 0.2 broadcast_compare_fusion.3
  88.7 2.8 %fusion.62 = (f32[4,512]{1,0:T(4,128)S(1)}, f32[512,512,4]{1,0,2:T(8,128)}) fusion(pred[512,512]{0,1:T(8,128)(4,1)S(1)} %broadcast_compare_fusion.3, bf16[512,1,4,64]{0,3,2,1:T(8,128)(2,1)S(1)} %get-tuple-element.393, bf16[2048,128]{0,1:T(8,128)(2,1)S(1)} %get-tuple-element.392, s32[]{:T(128)S(6)} %select_n.256), kind=kOutput, calls=%fused_computation.2.clone.1 | convolution fusion | flops 137361408 | bytes 4792324 | tf_op jit(solution)/shard_map/while/body/eval_jaxpr/qhgd,khd->hgqk/dot_general | solution.py:60
  91.5 0.0 copy-start
  91.5 3.7 %fusion.65 = f32[1,4,512,64]{2,3,1,0:T(8,128)S(1)} fusion(f32[512,512,4]{1,0,2:T(8,128)} %get-tuple-element.358, f32[4,512]{1,0:T(4,128)S(1)} %bitcast.99, pred[512,512]{0,1:T(8,128)(4,1)S(1)} %broadcast_compare_fusion.3, f32[1,4,512,64]{2,3,1,0:T(8,128)S(1)} %get-tuple-element.376, f32[4,512]{1,0:T(4,128)S(1)} %get-tuple-element.359, ...), kind=kOutput, calls=%fused_computation.9.clone.1 | convolution fusion | flops 139853824 | bytes 5586953 | tf_op jit(solution)/shard_map/while/body/eval_jaxpr/hgqk,khd->hgqd/dot_general | solution.py:69
  95.2 0.0 copy-done
  95.3 1.0 fusion.64
  96.3 0.1 fusion.35
  96.4 0.3 convert_element_type.40
  96.7 0.3 copy.15
  97.0 9.4 %all_to_all.16 = bf16[8,64,256]{2,1,0:T(8,128)(2,1)S(1)} all-to-all(bf16[8,64,256]{2,1,0:T(8,128)(2,1)S(1)} %copy.15), channel_id=1, replica_groups=mesh['grp'=4,'sp'=8] {'sp'}, dimensions={0} | all-to-all | bytes 524288 | tf_op jit(solution)/shard_map/all_to_all | solution.py:129
  106.5 0.7 copy.18
  (31 shorter events, 0.4 us)
Async XLA Ops:
  6.5 37.1 %all-gather.2.cloned.1.call-start = ((), (), s32[]{:S(2)}) async-start(), calls=%async_computation.1 | async-start | bytes 3391488 | tf_op jit(solution)/shard_map/all_gather | solution.py:97
  43.6 20.8 %copy-start.1 = (s32[16]{0:T(128)S(1)}, s32[16]{0:T(128)}, u32[]{:S(2)}) copy-start(s32[16]{0:T(128)} %param.10) | copy-start | bytes 196
  67.5 3.7 %copy-start = (f32[512,512,4]{1,0,2:T(8,128)S(1)}, f32[512,512,4]{1,0,2:T(8,128)}, u32[]{:S(2)}) copy-start(f32[512,512,4]{1,0,2:T(8,128)} %get-tuple-element.358) | copy-start | bytes 12582916 | tf_op jit(solution)/shard_map/while
  75.5 3.7 %copy-start = (f32[512,512,4]{1,0,2:T(8,128)S(1)}, f32[512,512,4]{1,0,2:T(8,128)}, u32[]{:S(2)}) copy-start(f32[512,512,4]{1,0,2:T(8,128)} %get-tuple-element.358) | copy-start | bytes 12582916 | tf_op jit(solution)/shard_map/while
  83.5 3.7 %copy-start = (f32[512,512,4]{1,0,2:T(8,128)S(1)}, f32[512,512,4]{1,0,2:T(8,128)}, u32[]{:S(2)}) copy-start(f32[512,512,4]{1,0,2:T(8,128)} %get-tuple-element.358) | copy-start | bytes 12582916 | tf_op jit(solution)/shard_map/while
  91.5 3.7 %copy-start = (f32[512,512,4]{1,0,2:T(8,128)S(1)}, f32[512,512,4]{1,0,2:T(8,128)}, u32[]{:S(2)}) copy-start(f32[512,512,4]{1,0,2:T(8,128)} %get-tuple-element.358) | copy-start | bytes 12582916 | tf_op jit(solution)/shard_map/while
Sparse Core Ops, SparseCore 0:
  9.2 34.3 all-gather.1
where the time goes:
time: 114 us
  waiting for transfers between devices  33.3 us (29%)
  matrix products  30.1 us (26%)
  blocking collectives  25.5 us (22%)
  between operations  13.6 us (12%)
  other arithmetic  7.27 us (6%)
  local copies, waits for them, and re-layouts  4.05 us (4%)
    all_gather x1, waiting for transfers between devices, per_device(): lax.all_gather(tokens, 'sp', axis=0, tiled=True)  32.6 us
    all_gather x1, blocking collectives, per_device(): piece = lax.all_gather(key_value_pair, 'grp', axis=0, tiled=True)  16 us
    dot_general x4, matrix products, attend(): jnp.einsum('hgqk,khd->hgqd', weights.astype(jnp.bfloat16), value_part, pr...  14.8 us
    dot_general x4, matrix products, attend(): jnp.einsum('qhgd,khd->hgqk', queries, key_part, preferred_element_type=jn...  11.2 us
    all_to_all x1, blocking collectives, per_device(): lax.all_to_all(attended, 'sp', split_axis=0, concat_axis=1, tiled=True)  9.44 us
    reduce_sum x4, other arithmetic, attend(): totals = totals * factor + jnp.sum(weights, axis=-1)  4.17 us
    dot_general x1, matrix products, per_device(): jnp.dot(lax.all_gather(tokens, 'sp', axis=0, tiled=True), joined, preferr...  4.11 us
  transfers between devices with their start and end apart: 1, of which 1 were waited for; matrix products, arithmetic and copies ran while one was open for 3% of the time, Pallas kernels for 0%

commit v1 on v0

v1 whole, which is shorter than its diff:
```python
import functools

import jax
import jax.numpy as jnp
from jax import lax
from jax.experimental import pallas as pl
from jax.experimental.pallas import tpu as pltpu
from jax.sharding import PartitionSpec as P

QUERY_HEADS = 32
HEAD_SIZE = 64
BPG = 4
LANES = 128

rope_base = 150000.0
neg_large = -1e30


def rotate_heads(x, cosine, sine):
    width = x.shape[1]
    half = HEAD_SIZE // 2
    if width % LANES:
        swapped = jnp.concatenate([x[:, half:], x[:, :half]], axis=1)
        return x * cosine[:, :width] + swapped * sine[:, :width]
    parts = []
    lane = lax.broadcasted_iota(jnp.int32, (x.shape[0], LANES), 1)
    first = lane % HEAD_SIZE < half
    for j in range(width // LANES):
        v = x[:, j * LANES : (j + 1) * LANES]
        swapped = jnp.where(first, pltpu.roll(v, LANES - half, 1), pltpu.roll(v, half, 1))
        parts.append(v * cosine + swapped * sine)
    return parts[0] if len(parts) == 1 else jnp.concatenate(parts, axis=1)


def kernel(
    grp, sp, qheads, kv_total,
    tok, wq_any, kvw_any, cos_ref, sin_ref, qpos, kpos, sink, out,
    toks, wq, wkv, kvb, q, abuf, obuf,
    wsem, tsend, tfwd, trecv, ksend, krecv, osend, orecv,
):
    s = lax.axis_index("sp")
    g = lax.axis_index("grp")
    rows = tok.shape[0]
    group_rows = rows * sp
    chips = sp // 2
    pair = 2 * rows
    qc = qheads * HEAD_SIZE
    c = s // 2
    par = s % 2
    partner = s + 1 - 2 * par
    head = s * kv_total // sp
    hpar = head % 2
    koff = pl.multiple_of(head // 2 * LANES, LANES)
    voff = pl.multiple_of(kv_total * HEAD_SIZE + head // 2 * LANES, LANES)

    wcopies = [
        pltpu.make_async_copy(wq_any, wq, wsem.at[0]),
        pltpu.make_async_copy(
            kvw_any.at[:, pl.ds(koff, LANES)], wkv.at[:, pl.ds(0, LANES)], wsem.at[1]
        ),
        pltpu.make_async_copy(
            kvw_any.at[:, pl.ds(voff, LANES)], wkv.at[:, pl.ds(LANES, LANES)], wsem.at[2]
        ),
    ]

    def send_tok(to):
        return pltpu.make_async_remote_copy(
            src_ref=tok, dst_ref=toks.at[s], send_sem=tsend.at[to], recv_sem=trecv.at[s],
            device_id={"sp": to},
        )

    def forward(slot):
        return pltpu.make_async_remote_copy(
            src_ref=toks.at[slot], dst_ref=toks.at[slot], send_sem=tfwd.at[slot],
            recv_sem=trecv.at[slot], device_id={"sp": partner},
        )

    def send_kv(chip, d):
        span = pl.ds(pl.multiple_of(g * group_rows + chip * pair, pair), pair)
        return pltpu.make_async_remote_copy(
            src_ref=kvb.at[span], dst_ref=kvb.at[span], send_sem=ksend.at[d, chip],
            recv_sem=krecv.at[g, chip], device_id={"grp": (g + d) % grp},
        )

    def recv_kv(chip, d):
        src = (g + d) % grp
        span = pl.ds(pl.multiple_of(src * group_rows + chip * pair, pair), pair)
        return pltpu.make_async_remote_copy(
            src_ref=kvb.at[span], dst_ref=kvb.at[span], send_sem=ksend.at[d, chip],
            recv_sem=krecv.at[src, chip], device_id={"grp": src},
        )

    def send_out(to):
        return pltpu.make_async_remote_copy(
            src_ref=abuf.at[to], dst_ref=obuf.at[s], send_sem=osend.at[to],
            recv_sem=orecv.at[s], device_id={"sp": to},
        )

    def recv_out(src):
        return pltpu.make_async_remote_copy(
            src_ref=abuf.at[src], dst_ref=obuf.at[src], send_sem=osend.at[src],
            recv_sem=orecv.at[src], device_id={"sp": src},
        )

    send_tok(partner).start()

    def start_tok(k, _):
        send_tok((c + k) % chips * 2 + par).start()
        return 0

    lax.fori_loop(1, chips, start_tok, 0)
    for copy in wcopies:
        copy.start()
    toks[s] = tok[...]
    for copy in wcopies:
        copy.wait()

    def project(k, _):
        chip = (c + chips - k) % chips

        @pl.when(k > 0)
        def _():
            slot = chip * 2 + par
            forward(slot).wait_recv()
            forward(slot).start()

        forward(chip * 2 + 1 - par).wait_recv()
        x = toks[pl.ds(chip * 2, 2)].reshape(pair, tok.shape[1])
        span = pl.ds(pl.multiple_of(chip * pair, pair), pair)
        cosine = cos_ref[span, :]
        sine = sin_ref[span, :]
        kv = jnp.dot(x, wkv[...], preferred_element_type=jnp.float32)
        keys = rotate_heads(kv[:, :LANES], cosine, sine)
        values = kv[:, LANES:]
        low = hpar == 0
        keys = jnp.where(low, keys, pltpu.roll(keys, HEAD_SIZE, 1))
        values = jnp.where(low, pltpu.roll(values, HEAD_SIZE, 1), values)
        lane = lax.broadcasted_iota(jnp.int32, (pair, LANES), 1)
        joined = jnp.where(lane < HEAD_SIZE, keys, values).astype(jnp.bfloat16)
        kvb[pl.ds(pl.multiple_of(g * group_rows + chip * pair, pair), pair), :] = joined
        for d in range(1, grp):
            send_kv(chip, d).start()
        qf = jnp.dot(x, wq[...], preferred_element_type=jnp.float32)
        qr = (rotate_heads(qf, cosine, sine) * HEAD_SIZE**-0.5).astype(jnp.bfloat16)
        zeros = jnp.zeros((pair, HEAD_SIZE), jnp.bfloat16)
        for h in range(qheads):
            q[h, span, :] = jnp.concatenate(
                [qr[:, h * HEAD_SIZE : (h + 1) * HEAD_SIZE], zeros], axis=1
            )
        return 0

    lax.fori_loop(0, chips, project, 0)

    def arrive(chip, _):
        for d in range(1, grp):
            recv_kv(chip, d).wait_recv()
        return 0

    lax.fori_loop(0, chips, arrive, 0)

    key_count = kvb.shape[0]
    chunk = min(key_count, 2048)
    chunks = key_count // chunk
    block = min(256, group_rows)
    tiles = block // rows

    def attention(b, _):
        span = pl.ds(pl.multiple_of(b * block, block), block)
        places = qpos[span, :]
        outs = []
        for h in range(qheads):
            qh = q[h, span, :]

            def visit(t, state):
                top, total, mix = state
                kspan = pl.ds(pl.multiple_of(t * chunk, chunk), chunk)
                kv = kvb[kspan, :]
                scores = lax.dot_general(
                    qh, kv, (((1,), (1,)), ((), ())), preferred_element_type=jnp.float32
                )
                allowed = kpos[:, kspan] <= places
                scores = jnp.where(allowed, scores, neg_large)
                higher = jnp.maximum(top, jnp.max(scores, axis=1, keepdims=True))
                weights = jnp.exp(scores - higher)
                factor = jnp.exp(top - higher)
                total = total * factor + jnp.sum(weights, axis=1, keepdims=True)
                mix = mix * factor + jnp.dot(
                    weights.astype(jnp.bfloat16), kv, preferred_element_type=jnp.float32
                )
                return higher, total, mix

            state = (
                jnp.full((block, 1), sink[s * qheads + h], jnp.float32),
                jnp.ones((block, 1), jnp.float32),
                jnp.zeros((block, LANES), jnp.float32),
            )
            if chunks == 1:
                state = visit(0, state)
            else:
                state = lax.fori_loop(0, chunks, visit, state)
            outs.append((state[2] / state[1])[:, HEAD_SIZE:])
        att = outs[0] if qheads == 1 else jnp.concatenate(outs, axis=1)
        abuf[pl.ds(b * tiles, tiles)] = att.astype(jnp.bfloat16).reshape(tiles, rows, qc)

        def ship(i, _):
            to = b * tiles + i

            @pl.when(to != s)
            def _():
                send_out(to).start()

            return 0

        lax.fori_loop(0, tiles, ship, 0)
        return 0

    lax.fori_loop(0, group_rows // block, attention, 0)
    obuf[s] = abuf[s]

    def drain(j, _):
        @pl.when(j != s)
        def _():
            recv_out(j).wait_recv()
            send_out(j).wait_send()

        return 0

    lax.fori_loop(0, sp, drain, 0)
    for j in range(sp):
        out[:, j * qc : (j + 1) * qc] = obuf[j]
    send_tok(partner).wait_send()

    def finish(k, _):
        send_tok((c + k) % chips * 2 + par).wait_send()
        forward((c + chips - k) % chips * 2 + par).wait_send()
        return 0

    lax.fori_loop(1, chips, finish, 0)

    def finish_kv(chip, _):
        for d in range(1, grp):
            send_kv(chip, d).wait_send()
        return 0

    lax.fori_loop(0, chips, finish_kv, 0)


def per_device(tokens, query_weight, key_value_weight, block_places, sinks):
    sp = lax.axis_size("sp")
    grp = lax.axis_size("grp")
    rows, width = tokens.shape
    group_rows = rows * sp
    block_rows = group_rows // BPG
    key_count = grp * group_rows
    qc = query_weight.shape[1]
    qheads = qc // HEAD_SIZE
    kv_total = key_value_weight.shape[1] // (2 * HEAD_SIZE)
    g = lax.axis_index("grp")

    within = jnp.arange(block_rows, dtype=jnp.int32)
    kpos = (block_places[:, None] * block_rows + within[None, :]).reshape(1, key_count)
    own = lax.dynamic_slice_in_dim(block_places, g * BPG, BPG, 0)
    qpos = (own[:, None] * block_rows + within[None, :]).reshape(group_rows, 1)
    freq = jnp.arange(HEAD_SIZE // 2, dtype=jnp.float32)
    inverse = rope_base ** (-(freq * 2.0) / HEAD_SIZE)
    lanes = jnp.tile(inverse, LANES // (HEAD_SIZE // 2))
    angles = qpos.astype(jnp.float32) * lanes[None, :]
    sign = jnp.where(jnp.arange(LANES) % HEAD_SIZE < HEAD_SIZE // 2, -1.0, 1.0)
    cosine = jnp.cos(angles)
    sine = jnp.sin(angles) * sign[None, :].astype(jnp.float32)

    vmem = pl.BlockSpec(memory_space=pltpu.VMEM)
    hbm = pl.BlockSpec(memory_space=pl.ANY)
    smem = pl.BlockSpec(memory_space=pltpu.SMEM)
    dma = pltpu.SemaphoreType.DMA
    return pl.pallas_call(
        functools.partial(kernel, grp, sp, qheads, kv_total),
        out_shape=jax.ShapeDtypeStruct((rows, qc * sp), jnp.bfloat16),
        in_specs=[vmem, hbm, hbm, vmem, vmem, vmem, vmem, smem],
        out_specs=vmem,
        scratch_shapes=[
            pltpu.VMEM((sp, rows, width), jnp.bfloat16),
            pltpu.VMEM((width, qc), jnp.bfloat16),
            pltpu.VMEM((width, 2 * LANES), jnp.bfloat16),
            pltpu.VMEM((key_count, LANES), jnp.bfloat16),
            pltpu.VMEM((qheads, group_rows, LANES), jnp.bfloat16),
            pltpu.VMEM((sp, rows, qc), jnp.bfloat16),
            pltpu.VMEM((sp, rows, qc), jnp.bfloat16),
            dma((3,)),
            dma((sp,)),
            dma((sp,)),
            dma((sp,)),
            dma((grp, sp // 2)),
            dma((grp, sp // 2)),
            dma((sp,)),
            dma((sp,)),
        ],
        compiler_params=pltpu.CompilerParams(
            has_side_effects=True, vmem_limit_bytes=60 * 1024 * 1024
        ),
    )(tokens, query_weight, key_value_weight, cosine, sine, qpos, kpos, sinks)


def solution(mesh):
    in_specs = (P(("grp", "sp"), None), P(None, "sp"), P(), P(), P())
    out_specs = P(("grp", "sp"), None)
    return jax.shard_map(
        per_device, mesh=mesh, in_specs=in_specs, out_specs=out_specs, check_vma=False
    )
```

time: 114 us -> 55.8 us (0.49)
  Pallas kernels: 0 us -> 49 us
  waiting for transfers between devices: 33.3 us -> 0 us
  matrix products: 30.1 us -> 0 us
  blocking collectives: 25.5 us -> 0 us
  between operations: 13.6 us -> 0.03 us
  other arithmetic: 7.27 us -> 3.94 us
  local copies, waits for them, and re-layouts: 4.05 us -> 2.6 us
    pallas_call x0 -> x1, Pallas kernels: none -> 49 us  [per_device(): pl.pallas_call(functools.partial(kernel, grp, sp, qheads, kv_total), out_...]
    all_gather x1 -> x0, waiting for transfers between devices: 32.6 us -> none  [per_device(): lax.all_gather(tokens, 'sp', axis=0, tiled=True)]
    dot_general x9 -> x0, matrix products: 30.1 us -> none  [the longest x4 14.8 us: attend(): jnp.einsum('hgqk,khd->hgqd', weights.astype(jnp.bfloat16), value_part, pr...]
    all_gather x1 -> x0, blocking collectives: 16 us -> none  [per_device(): piece = lax.all_gather(key_value_pair, 'grp', axis=0, tiled=True)]
    all_to_all x1 -> x0, blocking collectives: 9.44 us -> none  [per_device(): lax.all_to_all(attended, 'sp', split_axis=0, concat_axis=1, tiled=True)]
    reduce_sum x9 -> x0, other arithmetic: 5.27 us -> none  [the longest x4 4.17 us: attend(): totals = totals * factor + jnp.sum(weights, axis=-1)]
    mul x4 -> x3, other arithmetic: 0.05 us -> 3.18 us  [the longest x1 1.8 us: per_device(): sine = jnp.sin(angles) * sign[None, :].astype(jnp.float32)]
    dynamic_slice x2 -> x0, local copies, waits for them, and re-layouts: 2.56 us -> none  [the longest x1 1.83 us: per_device(): lax.dynamic_slice_in_dim(key_value_weight, first_head * HEAD_SIZE, kv_col...]
  transfers between devices with their start and end apart: 1 -> 0, of which waited for: 1 -> 0; matrix products, arithmetic and copies ran while one was open for 3% -> 0% of each run, Pallas kernels for 0% -> 0%
where the time goes in v1:
time: 55.8 us; the launch traced here: 55.6 us
  Pallas kernels  49 us (88%)
  other arithmetic  3.94 us (7%)
  local copies, waits for them, and re-layouts  2.6 us (5%)
    pallas_call x1, Pallas kernels, per_device(): pl.pallas_call(functools.partial(kernel, grp, sp, qheads, kv_total), out_...  49 us
    mul x1, other arithmetic, per_device(): sine = jnp.sin(angles) * sign[None, :].astype(jnp.float32)  1.8 us
    unnamed x1, local copies, waits for them, and re-layouts  1.67 us

profile of v1, /device:TPU:0, one launch (start us, length us, event | category | flops | bytes accessed | tf_op | source)
XLA Modules:
  0.0 55.6 jit_solution(7266754776183810287)
XLA Ops:
  0.0 0.7 %dynamic-slice_multiply_fusion = s32[4]{0:T(128)S(1)} fusion(s32[16]{0:T(128)} %param.8, s32[]{:T(128)S(6)} %select_n.22), kind=kLoop, calls=%fused_computation.9 | loop fusion | flops 4 | bytes 36 | tf_op jit(solution)/shard_map/mul | solution.py:263
  0.7 0.7 %broadcast_multiply_fusion = s32[16]{0:T(128)S(1)} fusion(s32[16]{0:T(128)} %param.8), kind=kLoop, calls=%fused_computation.10 | loop fusion | flops 16 | bytes 128 | tf_op jit(solution)/shard_map/mul | solution.py:261
  1.4 0.1 mul.49
  1.5 0.1 iota_add_fusion.1
  1.6 0.7 %iota_add_fusion = s32[16,128]{1,0:T(8,128)} fusion(s32[16]{0:T(128)S(1)} %broadcast_multiply_fusion), kind=kLoop, calls=%fused_computation.3 | loop fusion | flops 2048 | bytes 8256 | tf_op jit(solution)/shard_map/add | solution.py:261
  2.2 0.8 %copy.6.qpos = s32[512,1]{1,0:T(8,128)} copy(s32[512,1]{0,1:T(1,128)S(1)} %bitcast.5) | data formatting | bytes 4096 | tf_op jit(solution)/shard_map/add | solution.py:263
  3.1 1.8 %fusion = (f32[512,128]{1,0:T(8,128)}, f32[512,128]{1,0:T(8,128)}) fusion(f32[128]{0:T(128)S(1)} %compare_select_fusion, f32[128]{0:T(128)S(1)} %mul.49, f32[512]{0:T(512)S(1)} %get-tuple-element.8), kind=kLoop, calls=%fused_computation.2 | loop fusion | flops 131072 | bytes 527360 | tf_op jit(solution)/shard_map/mul | solution.py:270
  4.9 49.0 %shard_map.55 = bf16[64,2048]{1,0:T(8,128)(2,1)} custom-call(bf16[64,2880]{1,0:T(8,128)(2,1)} %tok.1, bf16[2880,256]{1,0:T(8,128)(2,1)} %wq_any.1, bf16[2880,1024]{1,0:T(8,128)(2,1)} %kvw_any.1, f32[512,128]{1,0:T(8,128)} %get-tuple-element.6.cos_ref, f32[512,128]{1,0:T(8,128)} %get-tuple-element.5.sin_ref, s32[512,1]{1,0:T(8,128)} %copy.6.qpos, ...), custom_call_target="tpu_custom_call" | custom-call | tf_op jit(solution)/shard_map/pallas_call | solution.py:276
  53.9 1.7 %copy.8 = bf16[64,2048]{1,0:T(8,128)(2,1)} copy(bf16[64,2048]{1,0:T(8,128)(2,1)} %shard_map.55) | data formatting | bytes 524288
  (3 shorter events, 0.0 us)

commit v2 on v1

--- a/solution.py
+++ b/solution.py
@@ -34,8 +34,8 @@
 
 def kernel(
     grp, sp, qheads, kv_total,
-    tok, wq_any, kvw_any, cos_ref, sin_ref, qpos, kpos, sink, out,
-    toks, wq, wkv, kvb, q, abuf, obuf,
+    tok, wq_any, kvw_any, inverse_ref, places_ref, sink, out,
+    toks, wq, wkv, kvb, q, abuf, obuf, cos_ref, sin_ref, qpos, kpos,
     wsem, tsend, tfwd, trecv, ksend, krecv, osend, orecv,
 ):
     s = lax.axis_index("sp")
@@ -112,6 +112,23 @@
     for copy in wcopies:
         copy.start()
     toks[s] = tok[...]
+
+    block_rows = group_rows // BPG
+    for j in range(kpos.shape[1] // block_rows):
+        within = lax.broadcasted_iota(jnp.int32, (1, block_rows), 1)
+        kpos[:, j * block_rows : (j + 1) * block_rows] = places_ref[j] * block_rows + within
+    wide = lax.broadcasted_iota(jnp.int32, (1, LANES), 1)
+    half = HEAD_SIZE // 2
+    inverse = inverse_ref[...]
+    sign = jnp.where(wide % HEAD_SIZE < half, -1.0, 1.0)
+    for j in range(BPG):
+        rspan = slice(j * block_rows, (j + 1) * block_rows)
+        within = lax.broadcasted_iota(jnp.int32, (block_rows, LANES), 0)
+        place = places_ref[g * BPG + j] * block_rows + within
+        qpos[rspan, :] = place[:, :1]
+        angles = place.astype(jnp.float32) * inverse
+        cos_ref[rspan, :] = jnp.cos(angles)
+        sin_ref[rspan, :] = jnp.sin(angles) * sign
     for copy in wcopies:
         copy.wait()
 
@@ -250,24 +267,13 @@
     grp = lax.axis_size("grp")
     rows, width = tokens.shape
     group_rows = rows * sp
-    block_rows = group_rows // BPG
     key_count = grp * group_rows
     qc = query_weight.shape[1]
     qheads = qc // HEAD_SIZE
     kv_total = key_value_weight.shape[1] // (2 * HEAD_SIZE)
-    g = lax.axis_index("grp")
-
-    within = jnp.arange(block_rows, dtype=jnp.int32)
-    kpos = (block_places[:, None] * block_rows + within[None, :]).reshape(1, key_count)
-    own = lax.dynamic_slice_in_dim(block_places, g * BPG, BPG, 0)
-    qpos = (own[:, None] * block_rows + within[None, :]).reshape(group_rows, 1)
     freq = jnp.arange(HEAD_SIZE // 2, dtype=jnp.float32)
     inverse = rope_base ** (-(freq * 2.0) / HEAD_SIZE)
-    lanes = jnp.tile(inverse, LANES // (HEAD_SIZE // 2))
-    angles = qpos.astype(jnp.float32) * lanes[None, :]
-    sign = jnp.where(jnp.arange(LANES) % HEAD_SIZE < HEAD_SIZE // 2, -1.0, 1.0)
-    cosine = jnp.cos(angles)
-    sine = jnp.sin(angles) * sign[None, :].astype(jnp.float32)
+    inverse = jnp.tile(inverse, LANES // (HEAD_SIZE // 2)).reshape(1, LANES)
 
     vmem = pl.BlockSpec(memory_space=pltpu.VMEM)
     hbm = pl.BlockSpec(memory_space=pl.ANY)
@@ -276,7 +282,7 @@
     return pl.pallas_call(
         functools.partial(kernel, grp, sp, qheads, kv_total),
         out_shape=jax.ShapeDtypeStruct((rows, qc * sp), jnp.bfloat16),
-        in_specs=[vmem, hbm, hbm, vmem, vmem, vmem, vmem, smem],
+        in_specs=[vmem, hbm, hbm, vmem, smem, smem],
         out_specs=vmem,
         scratch_shapes=[
             pltpu.VMEM((sp, rows, width), jnp.bfloat16),
@@ -286,6 +292,10 @@
             pltpu.VMEM((qheads, group_rows, LANES), jnp.bfloat16),
             pltpu.VMEM((sp, rows, qc), jnp.bfloat16),
             pltpu.VMEM((sp, rows, qc), jnp.bfloat16),
+            pltpu.VMEM((group_rows, LANES), jnp.float32),
+            pltpu.VMEM((group_rows, LANES), jnp.float32),
+            pltpu.VMEM((group_rows, 1), jnp.int32),
+            pltpu.VMEM((1, key_count), jnp.int32),
             dma((3,)),
             dma((sp,)),
             dma((sp,)),
@@ -298,7 +308,7 @@
         compiler_params=pltpu.CompilerParams(
             has_side_effects=True, vmem_limit_bytes=60 * 1024 * 1024
         ),
-    )(tokens, query_weight, key_value_weight, cosine, sine, qpos, kpos, sinks)
+    )(tokens, query_weight, key_value_weight, inverse, block_places, sinks)
 
 
 def solution(mesh):

time: 55.8 us -> 51.8 us (0.928)
  other arithmetic: 3.94 us -> 0.01 us
    mul x3 -> x0, other arithmetic: 3.18 us -> none  [the longest x1 1.8 us: per_device(): sine = jnp.sin(angles) * sign[None, :].astype(jnp.float32)]
    add x1 -> x0, local copies, waits for them, and re-layouts: 0.85 us -> none  [per_device(): qpos = (own[:, None] * block_rows + within[None, :]).reshape(group_rows, 1)]
    add x2 -> x0, other arithmetic: 0.74 us -> none  [the longest x1 0.67 us: per_device(): block_places[:, None] * block_rows + within[None, :]]
    another operation x1 -> x2, local copies, waits for them, and re-layouts: 0.01 us -> 0.61 us  [per_device(): inverse = jnp.tile(inverse, LANES // (HEAD_SIZE // 2)).reshape(1, LANES)]
where the time goes in v2:
time: 51.8 us; the launch traced here: 51.6 us
  Pallas kernels  49.3 us (95%)
  local copies, waits for them, and re-layouts  2.28 us (4%)
    pallas_call x1, Pallas kernels, per_device(): pl.pallas_call(functools.partial(kernel, grp, sp, qheads, kv_total), out_...  49.3 us
    unnamed x1, local copies, waits for them, and re-layouts  1.67 us

profile of v2, /device:TPU:0, one launch (start us, length us, event | category | flops | bytes accessed | tf_op | source)
XLA Modules:
  0.0 51.6 jit_solution(9789056555557980942)
XLA Ops:
  0.0 0.6 %reshape_tile.3.inverse_ref = f32[1,128]{1,0:T(1,128)} reshape(f32[4,32]{1,0:T(4,128)S(1)} %tile.2) | data formatting | bytes 1024 | tf_op jit(solution)/shard_map/reshape;tile | solution.py:276
  0.6 49.3 %shard_map.55 = bf16[64,2048]{1,0:T(8,128)(2,1)} custom-call(bf16[64,2880]{1,0:T(8,128)(2,1)} %tok.1, bf16[2880,256]{1,0:T(8,128)(2,1)} %wq_any.1, bf16[2880,1024]{1,0:T(8,128)(2,1)} %kvw_any.1, f32[1,128]{1,0:T(1,128)} %reshape_tile.3.inverse_ref, s32[16]{0:T(128)} %places_ref.1, f32[32]{0:T(128)} %sink.1), custom_call_target="tpu_custom_call" | custom-call | tf_op jit(solution)/shard_map/pallas_call | solution.py:282
  49.9 1.7 %copy.7 = bf16[64,2048]{1,0:T(8,128)(2,1)} copy(bf16[64,2048]{1,0:T(8,128)(2,1)} %shard_map.55) | data formatting | bytes 524288
  (2 shorter events, 0.0 us)

commit v3 on v2

--- a/solution.py
+++ b/solution.py
@@ -181,7 +181,10 @@
     block = min(256, group_rows)
     tiles = block // rows
 
-    def attention(b, _):
+    blocks = group_rows // block
+
+    def attention(turn, _):
+        b = (s // tiles + 1 + turn) % blocks
         span = pl.ds(pl.multiple_of(b * block, block), block)
         places = qpos[span, :]
         outs = []
@@ -231,7 +234,7 @@
         lax.fori_loop(0, tiles, ship, 0)
         return 0
 
-    lax.fori_loop(0, group_rows // block, attention, 0)
+    lax.fori_loop(0, blocks, attention, 0)
     obuf[s] = abuf[s]
 
     def drain(j, _):

time: 51.8 us -> 51.8 us (level)
  no operation moved by 1% of the time
where the time goes in v3:
time: 51.8 us; the launch traced here: 51.6 us
  Pallas kernels  49.3 us (95%)
  local copies, waits for them, and re-layouts  2.28 us (4%)
    pallas_call x1, Pallas kernels, per_device(): pl.pallas_call(functools.partial(kernel, grp, sp, qheads, kv_total), out_...  49.3 us
    unnamed x1, local copies, waits for them, and re-layouts  1.67 us

profile of v3, /device:TPU:0, one launch (start us, length us, event | category | flops | bytes accessed | tf_op | source)
XLA Modules:
  0.0 51.6 jit_solution(9853835793291339465)
XLA Ops:
  0.0 0.6 %reshape_tile.3.inverse_ref = f32[1,128]{1,0:T(1,128)} reshape(f32[4,32]{1,0:T(4,128)S(1)} %tile.2) | data formatting | bytes 1024 | tf_op jit(solution)/shard_map/reshape;tile | solution.py:279
  0.6 49.3 %shard_map.55 = bf16[64,2048]{1,0:T(8,128)(2,1)} custom-call(bf16[64,2880]{1,0:T(8,128)(2,1)} %tok.1, bf16[2880,256]{1,0:T(8,128)(2,1)} %wq_any.1, bf16[2880,1024]{1,0:T(8,128)(2,1)} %kvw_any.1, f32[1,128]{1,0:T(1,128)} %reshape_tile.3.inverse_ref, s32[16]{0:T(128)} %places_ref.1, f32[32]{0:T(128)} %sink.1), custom_call_target="tpu_custom_call" | custom-call | tf_op jit(solution)/shard_map/pallas_call | solution.py:285
  49.9 1.7 %copy.7 = bf16[64,2048]{1,0:T(8,128)(2,1)} copy(bf16[64,2048]{1,0:T(8,128)(2,1)} %shard_map.55) | data formatting | bytes 524288
  (2 shorter events, 0.0 us)

commit v4 on v3

--- a/solution.py
+++ b/solution.py
@@ -135,11 +135,18 @@
     def project(k, _):
         chip = (c + chips - k) % chips
 
-        @pl.when(k > 0)
-        def _():
-            slot = chip * 2 + par
+        def relay(turn):
+            slot = (c + chips - turn) % chips * 2 + par
             forward(slot).wait_recv()
             forward(slot).start()
+
+        @pl.when(k == 1)
+        def _():
+            relay(k)
+
+        @pl.when(jnp.logical_and(k > 0, k + 1 < chips))
+        def _():
+            relay(k + 1)
 
         forward(chip * 2 + 1 - par).wait_recv()
         x = toks[pl.ds(chip * 2, 2)].reshape(pair, tok.shape[1])

time: 51.8 us -> 52.9 us (1.021)
  Pallas kernels: 49.3 us -> 50.4 us
    pallas_call x1, Pallas kernels: 49.3 us -> 50.4 us  [per_device(): pl.pallas_call(functools.partial(kernel, grp, sp, qheads, kv_total), out_...]
where the time goes in v4:
time: 52.9 us; the launch traced here: 52.7 us
  Pallas kernels  50.4 us (95%)
  local copies, waits for them, and re-layouts  2.28 us (4%)
    pallas_call x1, Pallas kernels, per_device(): pl.pallas_call(functools.partial(kernel, grp, sp, qheads, kv_total), out_...  50.4 us
    unnamed x1, local copies, waits for them, and re-layouts  1.67 us

profile of v4, /device:TPU:0, one launch (start us, length us, event | category | flops | bytes accessed | tf_op | source)
XLA Modules:
  0.0 52.7 jit_solution(9677968136875016736)
XLA Ops:
  0.0 0.6 %reshape_tile.3.inverse_ref = f32[1,128]{1,0:T(1,128)} reshape(f32[4,32]{1,0:T(4,128)S(1)} %tile.2) | data formatting | bytes 1024 | tf_op jit(solution)/shard_map/reshape;tile | solution.py:286
  0.6 50.4 %shard_map.55 = bf16[64,2048]{1,0:T(8,128)(2,1)} custom-call(bf16[64,2880]{1,0:T(8,128)(2,1)} %tok.1, bf16[2880,256]{1,0:T(8,128)(2,1)} %wq_any.1, bf16[2880,1024]{1,0:T(8,128)(2,1)} %kvw_any.1, f32[1,128]{1,0:T(1,128)} %reshape_tile.3.inverse_ref, s32[16]{0:T(128)} %places_ref.1, f32[32]{0:T(128)} %sink.1), custom_call_target="tpu_custom_call" | custom-call | tf_op jit(solution)/shard_map/pallas_call | solution.py:292
  51.0 1.7 %copy.7 = bf16[64,2048]{1,0:T(8,128)(2,1)} copy(bf16[64,2048]{1,0:T(8,128)(2,1)} %shard_map.55) | data formatting | bytes 524288
  (2 shorter events, 0.0 us)
